TPU v7x, 32 devices: a whole 2x2x4 slice. The times are simulated.
32 devices in a mesh: group: 4 (over y, core), rep: 8 (over z, x).
Axes of the slice: x: 2, y: 2, z: 4, core: 2. Of those that a mesh axis runs over, the one named last changes fastest.
Arguments:
- table_hot: bfloat16 [32768, 512], P(('group', 'rep')), may hold values from -6 to 6
- table_mid: bfloat16 [131072, 128], P(('group', 'rep')), may hold values from -6 to 6
- table_cold: bfloat16 [131072, 128], P(('group', 'rep')), may hold values from -6 to 6
- proj_hot: bfloat16 [512, 256], replicated, may hold values from -0.25 to 0.25
- proj_mid: bfloat16 [128, 256], replicated, may hold values from -0.5 to 0.5
- proj_cold: bfloat16 [32, 256], replicated, may hold values from -1 to 1
- tower_in: bfloat16 [256, 1024], replicated, may hold values from -0.375 to 0.375
- tower_out: bfloat16 [1024, 256], replicated, may hold values from -0.1875 to 0.1875
- queries: bfloat16 [16384, 256], P(('group', 'rep')), may hold values from -68 to 68
- labels: int32 [16384], P(('group', 'rep')), may hold values from 0 to 4095
- item_slot: int32 [32, 4, 1024], P(('group', 'rep')), may hold values from 0 to 255
- item_block: int32 [32, 4, 1024], P(('group', 'rep')), may hold values from 0 to 2
- serve_rows: int32 [32, 3, 256], P(('group', 'rep')), may hold values from 0 to 16383, as said below
Outputs:
- query_loss: float32 [16384], P(('group', 'rep'))
- query_grad: float32 [16384, 256], P(('group', 'rep'))
- grad_hot: float32 [32768, 512], P(('group', 'rep'))
- grad_mid: float32 [131072, 128], P(('group', 'rep'))
- grad_cold: float32 [131072, 128], P(('group', 'rep'))
- grad_proj_hot: float32 [512, 256], P(None, 'rep')
- grad_proj_mid: float32 [128, 256], P(None, 'rep')
- grad_proj_cold: float32 [32, 256], P(None, 'rep')
- grad_tower_in: float32 [256, 1024], P(None, 'rep')
- grad_tower_out: float32 [1024, 256], P(None, 'rep')
Inputs may be any that keep to these rules, and one draw needn't show every extreme that they name: serve_rows[o, b, d * 8 + c] is a row of owner o's shard of block b that requester d sees in slot c; for block 0 it is below 1024, for block 1 below 4096, for block 2 below 16384; the 8 rows that one owner serves to one requester in one block are distinct.
All inputs are finite; a program needn't handle non-finite values.
Results may differ from a plain program's by a relative error of at most 0.02.
The roundings to bfloat16 on the way count: a program that leaves them out, or rounds other values in their place, can miss the bound.
Values may be sent and summed in bfloat16 or wider, within the bound.
No kernel may reach another device: no remote copies, remote signals or barrier semaphores. Data moves between devices by JAX's collectives and lax.ppermute only.
A program may use at most 128 MiB of HBM per device.

v0:
```python
import functools

import jax
import jax.numpy as jnp
from jax import lax
from jax.experimental import pallas as pl
from jax.experimental.pallas import tpu as pltpu
from jax.sharding import PartitionSpec as P


NORM_EPS = 1e-06
LOGIT_SCALE = 0.2
LOG2_E = 1.4426950408889634
AXES = ("group", "rep")
LANES = 128
QB = 256
IB = 256
MIB = 1 << 20
F32 = jnp.float32
BF16 = jnp.bfloat16

NN = (((1,), (0,)), ((), ()))
NT = (((1,), (1,)), ((), ()))
TN = (((0,), (0,)), ((), ()))


def mm(left, right, dims=NN):
    return lax.dot_general(left, right, dims, preferred_element_type=F32)


def ones_where(mask):
    return jnp.where(mask, jnp.float32(1), jnp.float32(0))


def iota(shape, dim):
    return lax.broadcasted_iota(jnp.int32, shape, dim)


def call(body, out_shape, inputs, far=(), scratch=(), vmem=40):
    spec = pl.BlockSpec(memory_space=pltpu.VMEM)
    return pl.pallas_call(
        body,
        out_shape=out_shape,
        in_specs=[spec] * len(inputs) + [pl.BlockSpec(memory_space=pltpu.HBM)] * len(far),
        out_specs=jax.tree.map(lambda _: spec, out_shape),
        scratch_shapes=list(scratch),
        compiler_params=pltpu.CompilerParams(vmem_limit_bytes=vmem * MIB),
    )(*inputs, *far)


def sds(shape, dtype):
    return jax.ShapeDtypeStruct(shape, dtype)


def columns_of(served, pad_ref):
    pad_ref[...] = jnp.zeros_like(pad_ref)
    for k in range(served.shape[0]):
        pad_ref[k : k + 1, :] = served[k]
    return pad_ref[...].T


def parts_of(shape, lanes):
    return max(1, lanes // shape[1])


def split_row(row, part):
    return lax.div(row, part), lax.rem(row, part)


def gather_body(cold_width, parts, served, hot, mid, cold, out, pad, asked, v_hot, v_mid, v_cold, sems):
    copies = [
        pltpu.make_async_copy(source, target, sems.at[k])
        for k, (source, target) in enumerate(
            ((served, asked), (hot, v_hot), (mid, v_mid), (cold, v_cold))
        )
    ]
    for copy in copies:
        copy.start()
    copies[0].wait()
    idx = columns_of(asked, pad)
    slots = out.shape[0]

    def pick(k, table, row, w):
        part = table.shape[0] // parts[k]
        which, low = split_row(row, part)
        hit = ones_where(iota((slots, part), 1) == low).astype(BF16)
        copies[k + 1].wait()
        wide = [table[p * part : (p + 1) * part, :] for p in range(parts[k])]
        found = mm(hit, wide[0] if parts[k] == 1 else jnp.concatenate(wide, axis=1))
        value = found[:, 0:w]
        for p in range(1, parts[k]):
            value = jnp.where(which == p, found[:, p * w : (p + 1) * w], value)
        return value

    w_hot, w_mid, w_cold = hot.shape[1], mid.shape[1], cold.shape[1]
    out[:, 0:w_hot] = pick(0, v_hot, idx[:, 0:1], w_hot).astype(BF16)
    out[:, w_hot : w_hot + w_mid] = pick(1, v_mid, idx[:, 1:2], w_mid).astype(BF16)
    row = idx[:, 2:3]
    lines = pick(2, v_cold, lax.shift_right_logical(row, 2), w_cold)
    mine = lax.div(iota(lines.shape, 1), cold_width) == (row & 3)
    out[:, w_hot + w_mid :] = jnp.where(mine, lines, 0.0).astype(BF16)


def gather_rows(served, table_hot, table_mid, table_cold, cold_width):
    slots = served.shape[2]
    tables = (table_hot, table_mid, table_cold)
    width = sum(table.shape[1] for table in tables)
    lanes = max(table.shape[1] for table in tables)
    parts = [parts_of(table.shape, lanes) for table in tables]
    hbm = pl.BlockSpec(memory_space=pltpu.HBM)
    vmem = pl.BlockSpec(memory_space=pltpu.VMEM)
    return pl.pallas_call(
        functools.partial(gather_body, cold_width, parts),
        out_shape=sds((slots, width), BF16),
        in_specs=[hbm, hbm, hbm, hbm],
        out_specs=vmem,
        scratch_shapes=[pltpu.VMEM((8, slots), jnp.int32), pltpu.VMEM(served.shape, jnp.int32)]
        + [pltpu.VMEM(table.shape, BF16) for table in tables]
        + [pltpu.SemaphoreType.DMA((4,))],
        compiler_params=pltpu.CompilerParams(vmem_limit_bytes=60 * MIB),
        name="gather_rows",
    )(served, *tables)


def slot_of(slots, item_slot, item_block):
    return item_block[0] * slots + item_slot[0]


def count_body(slots, item_slot, item_block, by_item, by_slot, pad):
    fields, items = item_slot.shape[1], item_slot.shape[2]
    which = slot_of(slots, item_slot, item_block)
    count_slots(which, by_slot)
    pad[...] = jnp.zeros_like(pad)
    pad[0:fields, :] = which
    cols = pad[...].T
    for base in range(0, by_item.shape[1], QB):
        lanes = iota((items, QB), 1) + base
        total = jnp.zeros((items, QB), F32)
        for f in range(fields):
            total += ones_where(lanes == cols[:, f : f + 1])
        by_item[:, base : base + QB] = total.astype(BF16)


def count_slots(which, by_slot):
    for base in range(0, by_slot.shape[0], QB):
        rows = iota((QB, which.shape[1]), 0) + base
        total = jnp.zeros((QB, which.shape[1]), F32)
        for f in range(which.shape[0]):
            total += ones_where(rows == which[f : f + 1, :])
        by_slot[base : base + QB, :] = total.astype(BF16)


def tall(weight, times):
    return jnp.concatenate([weight] * times, axis=0)


def label_rows(label, base, jj):
    row = label[0:1, jj * QB : (jj + 1) * QB] - base
    return row - iota((8, QB), 0)


def hits(rows, label, at):
    first = 8 * iota((rows // 8, 8, QB), 0) + at
    return first == label[None]


def by_eight(value):
    return value.reshape(value.shape[0] // 8, 8, value.shape[1])


def sigmoid(value):
    return 0.5 + 0.5 * jnp.tanh(0.5 * value)


def forward_body(peers, raw, counts, p_hot, p_mid, p_cold, t_in, t_out, *rest):
    queries, labels = rest[:peers], rest[peers : 2 * peers]
    pooled_o, resid_o, vec_o, stats_o, tops_o, exp_o, table = rest[2 * peers :]
    slots = raw.shape[0]
    w_hot, w_mid = p_hot.shape[0], p_mid.shape[0]
    w_cold = raw.shape[1] - w_hot - w_mid
    table[0:slots, :] = mm(raw[:, 0:w_hot], p_hot[...]).astype(BF16)
    table[slots : 2 * slots, :] = mm(raw[:, w_hot : w_hot + w_mid], p_mid[...]).astype(BF16)
    table[2 * slots :, :] = mm(
        raw[:, w_hot + w_mid :], tall(p_cold[...], w_cold // p_cold.shape[0])
    ).astype(BF16)
    items = counts.shape[0]
    base = lax.axis_index("group") * items
    nq = queries[0].shape[0]
    per = nq // QB
    blocks = [(t, jj) for t in range(peers) for jj in range(per)]
    wanted = [label_rows(labels[t], base, jj) for t, jj in blocks]
    kept = [[] for _ in blocks]
    step = t_in.shape[1] // 4

    def tower(ib):
        rows = slice(ib * IB, (ib + 1) * IB)
        pooled = mm(counts[rows, :], table[...]).astype(BF16)
        pooled_o[rows, :] = pooled
        resid = pooled.astype(F32)
        yield
        for at in range(0, t_in.shape[1], step):
            pre = mm(pooled, t_in[:, at : at + step])
            hidden = (pre * sigmoid(pre)).astype(BF16)
            yield
            resid += mm(hidden, t_out[at : at + step, :])
        inv = lax.rsqrt(jnp.mean(resid * resid, axis=1, keepdims=True) + NORM_EPS)
        resid_o[rows, :] = resid
        vec_o[rows, :] = (resid * inv).astype(BF16)

    def score(ib, j):
        at = ib * IB
        rows = slice(at, at + IB)
        t, jj = blocks[j]
        s = mm(vec_o[rows, :], queries[t][jj * QB : (jj + 1) * QB, :], NT)
        top = jnp.max(s, axis=0, keepdims=True)
        grown = jnp.exp2((s - top) * (LOGIT_SCALE * LOG2_E))
        total = jnp.sum(grown, axis=0, keepdims=True)
        picked = jnp.where(hits(IB, wanted[j], at), by_eight(s), 0.0)
        picked = jnp.sum(jnp.sum(picked, axis=0), axis=0, keepdims=True)
        exp_o[rows, j * QB : (j + 1) * QB] = grown
        top = LOGIT_SCALE * top
        tops_o[j : j + 1, ib * QB : (ib + 1) * QB] = top
        kept[j].append((top, total, LOGIT_SCALE * picked))

    for _ in tower(0):
        pass
    for ib in range(items // IB):
        ahead = tower(ib + 1) if ib + 1 < items // IB else iter(())
        for j in range(len(blocks)):
            next(ahead, None)
            score(ib, j)
        for _ in ahead:
            pass
    for j, parts in enumerate(kept):
        top = functools.reduce(jnp.maximum, [part[0] for part in parts])
        stats_o[j : j + 1, 0:QB] = top
        stats_o[j : j + 1, QB : 2 * QB] = sum(p[1] * jnp.exp(p[0] - top) for p in parts)
        stats_o[j : j + 1, 2 * QB :] = sum(part[2] for part in parts)


def slope_body(pooled, t_in, hidden_o, slope_o):
    for at in range(0, pooled.shape[0], IB):
        rows = slice(at, at + IB)
        pre = mm(pooled[rows, :], t_in[...])
        sig = sigmoid(pre)
        hidden_o[rows, :] = (pre * sig).astype(BF16)
        slope_o[rows, :] = sig * (1.0 + pre * (1.0 - sig))


class Plan:
    def __init__(self, groups, reps, width, inner, raw_width):
        self.groups, self.reps = groups, reps
        self.ky = groups // 2
        self.kx, self.kz = 2, reps // 2
        self.hr = inner // reps
        self.dr = width // reps
        self.b_in = width // LANES
        self.b_out = inner // LANES
        self.b_raw = raw_width // LANES
        rows = self.hr * self.b_in + self.dr * (self.b_out + self.b_raw)
        unit = 16 * self.ky
        units = -(-rows // (2 * unit))
        self.half = units * unit
        self.m1 = -(-units // 2) * 16
        self.m2 = units * 16 - self.m1
        self.rows = 2 * self.half
        self.used = rows
        self.p1 = reps * self.ky * self.m1
        self.p2 = reps * self.ky * self.m2


def backward_body(plan, peers, *refs):
    stats, refs = refs[:peers], refs[peers:]
    queries, refs = refs[:peers], refs[peers:]
    labels, refs = refs[:peers], refs[peers:]
    tops_r, grown, hidden, slope, resid, pooled, by_slot, raw = refs[:8]
    p_hot, p_mid, p_cold, t_in, t_out = refs[8:13]
    loss_o, grad_o, keep_o, send_o, back_o = refs[13:18]
    low_s, pre_s, pgrad_s, slot_s, chunk = refs[18:]
    items, width = pooled.shape
    nq = queries[0].shape[0]
    per = nq // QB
    me_g, me_r = lax.axis_index("group"), lax.axis_index("rep")
    base = me_g * items
    log_totals, wanted = [], []
    for t in range(peers):
        for jj in range(per):
            rows = [(t ^ s) * per + jj for s in range(peers)]
            tops = [stats[s][rows[s] : rows[s] + 1, 0:QB] for s in range(peers)]
            totals = [stats[s][rows[s] : rows[s] + 1, QB : 2 * QB] for s in range(peers)]
            top = functools.reduce(jnp.maximum, tops)
            total = sum(tot * jnp.exp(m - top) for m, tot in zip(tops, totals))
            log_total = top + jnp.log(total)
            if t == 0:
                picked = sum(stats[s][rows[s] : rows[s] + 1, 2 * QB :] for s in range(peers))
                loss_o[0:1, jj * QB : (jj + 1) * QB] = log_total - picked
            log_totals.append(log_total)
            wanted.append(label_rows(labels[t], base, jj))
    for at in range(0, items, IB):
        rows = slice(at, at + IB)
        for j, log_total in enumerate(log_totals):
            ib = at // IB
            scale = jnp.exp(tops_r[j : j + 1, ib * QB : (ib + 1) * QB] - log_total)
            share = by_eight(grown[rows, j * QB : (j + 1) * QB] * scale)
            share = share - ones_where(hits(IB, wanted[j], at))
            grad_o[rows, j * QB : (j + 1) * QB] = share.reshape(IB, QB).astype(BF16)
        vgrad = mm(grad_o[rows, 0:nq], queries[0][...])
        for t in range(1, peers):
            vgrad += mm(grad_o[rows, t * nq : (t + 1) * nq], queries[t][...])
        vgrad = LOGIT_SCALE * vgrad
        res = resid[rows, :]
        inv = lax.rsqrt(jnp.mean(res * res, axis=1, keepdims=True) + NORM_EPS)
        dot_wide = jnp.sum(vgrad * res, axis=1, keepdims=True)
        wide = inv * vgrad - (inv * inv * inv / width * dot_wide) * res
        low = wide.astype(BF16)
        low_s[rows, :] = low
        pre_g = (mm(low, t_out[...], NT) * slope[rows, :]).astype(BF16)
        pre_s[rows, :] = pre_g
        pgrad_s[rows, :] = (mm(pre_g, t_in[...], NT) + wide).astype(BF16)
    slots = raw.shape[0]
    w_hot, w_mid = p_hot.shape[0], p_mid.shape[0]
    w_cold = raw.shape[1] - w_hot - w_mid
    slot_s[...] = mm(by_slot[...], pgrad_s[...]).astype(BF16)
    back_o[:, 0:width] = slot_s[0:slots, :]
    back_o[:, width : width + w_mid] = mm(slot_s[slots : 2 * slots, :], p_mid[...], NT).astype(BF16)
    back_o[:, width + w_mid :] = mm(
        slot_s[2 * slots :, :], tall(p_cold[...], w_cold // p_cold.shape[0]), NT
    ).astype(BF16)

    g_in = mm(pooled[...], pre_s[...], TN).T
    hr, dr = plan.hr, plan.dr
    for r in range(plan.reps):
        for b in range(plan.b_in):
            chunk[r, b * hr : (b + 1) * hr, :] = g_in[
                r * hr : (r + 1) * hr, b * LANES : (b + 1) * LANES
            ].astype(BF16)
    at = hr * plan.b_in
    g_out = mm(low_s[...], hidden[...], TN)
    parts = [(g_out, plan.b_out)]
    lane = 0
    for b, w in enumerate((w_hot, w_mid, w_cold)):
        parts.append(
            (mm(slot_s[b * slots : (b + 1) * slots, :], raw[:, lane : lane + w], TN), w // LANES)
        )
        lane += w
    for value, blocks in parts:
        for r in range(plan.reps):
            for b in range(blocks):
                chunk[r, at + b * dr : at + (b + 1) * dr, :] = value[
                    r * dr : (r + 1) * dr, b * LANES : (b + 1) * LANES
                ].astype(BF16)
        at += blocks * dr
    if plan.rows > plan.used:
        chunk[:, plan.used :, :] = jnp.zeros((plan.reps, plan.rows - plan.used, LANES), BF16)
    core, me_y = me_g & 1, lax.shift_right_logical(me_g, 1)
    for h, out in ((0, keep_o), (1, send_o)):
        start = (core ^ h) * plan.half
        for z in range(plan.kz):
            for x in range(plan.kx):
                r = me_r ^ (z * 2 + x)
                for y in range(plan.ky):
                    q = me_y ^ y
                    m = plan.m1
                    at = ((x * plan.ky + y) * plan.kz + z) * m
                    row = pl.multiple_of(start + q * m, 16)
                    out[at : at + m, :] = chunk[r, pl.ds(row, m), :]
                    m = plan.m2
                    if m:
                        at = plan.p1 + ((y * plan.kx + x) * plan.kz + z) * m
                        row = pl.multiple_of(start + plan.ky * plan.m1 + q * m, 16)
                        out[at : at + m, :] = chunk[r, pl.ds(row, m), :]


def query_grad_body(peers, vec, grad, keep_o, send_o):
    turned = vec[...].T
    nq = keep_o.shape[2]
    for t in range(peers):
        part = (LOGIT_SCALE * mm(turned, grad[:, t * nq : (t + 1) * nq])).astype(BF16)
        (send_o if t & 1 else keep_o)[t // 2] = part


def query_core_body(keep, got, own_o, *sends):
    own_o[...] = keep[0].astype(F32) + got[0].astype(F32)
    for y, out in enumerate(sends):
        out[...] = (keep[y + 1].astype(F32) + got[y + 1].astype(F32)).astype(BF16)


def query_final_body(own, *rest):
    got, out = rest[:-1], rest[-1]
    total = own[...]
    for part in got:
        total += part[...].astype(F32)
    out[...] = total.T


def cut_body(cuts, *refs):
    n_in = len(refs) - len(cuts)
    for out, pieces in zip(refs[n_in:], cuts):
        for at, rows, terms in pieces:
            total = None
            for i, first in terms:
                part = refs[i][first : first + rows, :].astype(F32)
                total = part if total is None else total + part
            out[at : at + rows, :] = total.astype(out.dtype)


def cut(inputs, cuts):
    shapes = [sds((sum(p[1] for p in pieces), LANES), BF16) for pieces in cuts]
    return call(functools.partial(cut_body, cuts), shapes, inputs, vmem=8)


def final_body(plan, w_hot, w_mid, w_cold, cold_rows, *refs):
    pieces = refs[: plan.groups]
    o_in, o_out, o_hot, o_mid, o_cold, chunk = refs[plan.groups :]
    me_g = lax.axis_index("group")
    for t in range(plan.groups):
        h = (me_g & 1) ^ (t & 1)
        q = lax.shift_right_logical(me_g, 1) ^ (t >> 1)
        start = h * plan.half
        row = pl.multiple_of(start + q * plan.m1, 16)
        chunk[pl.ds(row, plan.m1), :] = pieces[t][0 : plan.m1, :].astype(F32)
        if plan.m2:
            row = pl.multiple_of(start + plan.ky * plan.m1 + q * plan.m2, 16)
            chunk[pl.ds(row, plan.m2), :] = pieces[t][plan.m1 :, :].astype(F32)
    hr, dr = plan.hr, plan.dr
    for b in range(plan.b_in):
        o_in[b * LANES : (b + 1) * LANES, :] = chunk[b * hr : (b + 1) * hr, :].T
    at = hr * plan.b_in
    for out, w in ((o_out, plan.b_out * LANES), (o_hot, w_hot), (o_mid, w_mid)):
        for b in range(w // LANES):
            out[:, b * LANES : (b + 1) * LANES] = chunk[at : at + dr, :]
            at += dr
    total = jnp.zeros((cold_rows, dr), F32)
    for _ in range(w_cold // LANES):
        turned = chunk[at : at + dr, :].T
        for k in range(LANES // cold_rows):
            total += turned[k * cold_rows : (k + 1) * cold_rows, :]
        at += dr
    o_cold[...] = total


def scatter_body(cold_width, rows_each, served, back, p_hot, *refs):
    outs, (pad, *wides), stages, sems = refs[:3], refs[3:7], refs[7:10], refs[10]
    width = p_hot.shape[1]
    slots = back.shape[0]
    w_mid, w_cold = outs[1].shape[1], outs[2].shape[1]
    cols = columns_of(served, pad)
    copies = []

    def widen(wide, row, part, values):
        w = values.shape[1]
        which = split_row(row, part)[0]
        for k in range(wide.shape[1] // w):
            wide[:, k * w : (k + 1) * w] = jnp.where(which == k, values, 0.0).astype(BF16)

    def put(out, stage, row, wide):
        w = out.shape[1]
        parts = wide.shape[1] // w
        part = out.shape[0] // parts
        low = split_row(row, part)[1]
        for at in range(0, part, rows_each):
            hit = ones_where(iota((rows_each, slots), 0) + at == low).astype(BF16)
            found = mm(hit, wide[...])
            for k in range(parts):
                rows = pl.ds(k * part + at, rows_each)
                stage[rows, :] = found[:, k * w : (k + 1) * w]
                copy = pltpu.make_async_copy(
                    stage.at[rows, :], out.at[rows, :], sems.at[len(copies)]
                )
                copy.start()
                copies.append(copy)

    wides[0][...] = mm(back[:, 0:width], p_hot[...], NT).astype(BF16)
    put(outs[0], stages[0], served[0], wides[0])
    mids = back[:, width : width + w_mid].astype(F32)
    widen(wides[1], cols[:, 1:2], outs[1].shape[0] * w_mid // wides[1].shape[1], mids)
    put(outs[1], stages[1], served[1], wides[1])
    lines = back[:, width + w_mid :].astype(F32)
    mine = lax.div(iota(lines.shape, 1), cold_width) == (cols[:, 2:3] & 3)
    row = lax.shift_right_logical(cols[:, 2:3], 2)
    part = outs[2].shape[0] * w_cold // wides[2].shape[1]
    widen(wides[2], row, part, jnp.where(mine, lines, 0.0))
    put(outs[2], stages[2], lax.shift_right_logical(served[2], 2), wides[2])
    for copy in copies:
        copy.wait()


def scatter_rows(served, back, proj_hot, shapes, cold_width):
    slots = served.shape[2]
    lanes = max(shape[1] for shape in shapes)
    parts = [parts_of(shape, lanes) for shape in shapes]
    rows_each = 256
    count = sum(shape[0] for shape in shapes) // rows_each
    vmem, hbm = pl.BlockSpec(memory_space=pltpu.VMEM), pl.BlockSpec(memory_space=pltpu.HBM)
    return pl.pallas_call(
        functools.partial(scatter_body, cold_width, rows_each),
        out_shape=[sds(shape, F32) for shape in shapes],
        in_specs=[vmem] * 3,
        out_specs=[hbm] * 3,
        scratch_shapes=[pltpu.VMEM((8, slots), jnp.int32)]
        + [pltpu.VMEM((slots, p * shape[1]), BF16) for p, shape in zip(parts, shapes)]
        + [pltpu.VMEM(shape, F32) for shape in shapes]
        + [pltpu.SemaphoreType.DMA((count,))],
        compiler_params=pltpu.CompilerParams(vmem_limit_bytes=24 * MIB),
        name="scatter_rows",
    )(served, back, proj_hot)


def local(
    groups,
    reps,
    table_hot,
    table_mid,
    table_cold,
    proj_hot,
    proj_mid,
    proj_cold,
    tower_in,
    tower_out,
    queries,
    labels,
    item_slot,
    item_block,
    serve_rows,
):
    devices = groups * reps
    slots = serve_rows.shape[2]
    cold_width, width = proj_cold.shape
    inner = tower_in.shape[1]
    items = item_slot.shape[2]
    nq = queries.shape[0]
    w_hot, w_mid, w_cold = table_hot.shape[1], table_mid.shape[1], table_cold.shape[1]
    raw_width = w_hot + w_mid + w_cold
    plan = Plan(groups, reps, width, inner, raw_width)

    def across_group(value, t):
        pairs = [(g * reps + r, (g ^ t) * reps + r) for g in range(groups) for r in range(reps)]
        return lax.ppermute(value, AXES, pairs)

    def across_rep(value, t):
        pairs = [(g * reps + r, g * reps + (r ^ t)) for g in range(groups) for r in range(reps)]
        return lax.ppermute(value, AXES, pairs)

    def to_all(rows):
        each = rows.reshape(devices, slots // devices, rows.shape[1])
        return lax.all_to_all(each, AXES, 0, 0, tiled=True).reshape(rows.shape)

    def to_group(value):
        found = {0: value}
        for t in range(2, groups, 2):
            found[t] = across_group(value, t)
        for t in range(0, groups, 2):
            found[t + 1] = across_group(found[t], 1)
        return [found[t] for t in range(groups)]

    served = jnp.transpose(serve_rows, (1, 0, 2))
    q_all = to_group(queries)
    rows = gather_rows(served, table_hot, table_mid, table_cold, cold_width)
    raw = to_all(rows)
    l_all = to_group(labels.reshape(1, nq))
    by_item, by_slot = call(
        functools.partial(count_body, slots),
        [sds((items, 3 * slots), BF16), sds((3 * slots, items), BF16)],
        [item_slot, item_block],
        scratch=[pltpu.VMEM((8, items), jnp.int32)],
        vmem=60,
    )
    blocks = groups * nq // QB
    pooled, resid, vec, stats, tops, grown = call(
        functools.partial(forward_body, groups),
        [
            sds((items, width), BF16),
            sds((items, width), F32),
            sds((items, width), BF16),
            sds((blocks, 3 * QB), F32),
            sds((blocks, items // IB * QB), F32),
            sds((items, groups * nq), F32),
        ],
        [raw, by_item, proj_hot, proj_mid, proj_cold, tower_in, tower_out] + q_all + l_all,
        scratch=[pltpu.VMEM((3 * slots, width), BF16)],
        vmem=8 * groups - 8,
    )
    s_all = [stats]
    for t in range(1, groups):
        s_all.append(across_group(stats, t))
    hidden, slope = call(
        slope_body,
        [sds((items, inner), BF16), sds((items, inner), F32)],
        [pooled, tower_in],
        vmem=12,
    )
    cut_rows = plan.p1 + plan.p2
    loss, grad, keep, send, back = call(
        functools.partial(backward_body, plan, groups),
        [
            sds((1, nq), F32),
            sds((items, groups * nq), BF16),
            sds((cut_rows, LANES), BF16),
            sds((cut_rows, LANES), BF16),
            sds((slots, width + w_mid + w_cold), BF16),
        ],
        s_all
        + q_all
        + l_all
        + [tops, grown, hidden, slope, resid, pooled, by_slot, raw]
        + [proj_hot, proj_mid, proj_cold, tower_in, tower_out],
        scratch=[
            pltpu.VMEM((items, width), BF16),
            pltpu.VMEM((items, inner), BF16),
            pltpu.VMEM((items, width), BF16),
            pltpu.VMEM((3 * slots, width), BF16),
            pltpu.VMEM((reps, plan.rows, LANES), BF16),
        ],
        vmem=8 * groups - 8,
    )
    back = to_all(back)

    got = across_group(send, 1)
    ky, kx, kz, m1, m2 = plan.ky, plan.kx, plan.kz, plan.m1, plan.m2

    n1, n2 = plan.p1 // kx, plan.p2 // ky
    cuts = []
    for x in range(kx):
        cuts.append([(0, n1, [(0, x * n1), (1, x * n1)])])
    for y in range(ky):
        cuts.append([(0, n2, [(0, plan.p1 + y * n2), (1, plan.p1 + y * n2)])])
    parts = cut([keep, got], cuts)
    a_keep, a_send = parts[0], parts[1:kx]
    b_keep, b_send = parts[kx], parts[kx + 1 :]
    a_got = [across_rep(v, x + 1) for x, v in enumerate(a_send)]
    b_got = [across_group(v, 2 * (y + 1)) for y, v in enumerate(b_send)]
    k1, k2 = n1 // ky, n2 // kx
    na, nb = 1 + len(a_got), 1 + len(b_got)
    cuts = [[(0, k1, [(i, y * k1) for i in range(na)])] for y in range(ky)]
    cuts += [[(0, k2, [(na + i, x * k2) for i in range(nb)])] for x in range(kx)]
    parts = cut([a_keep, *a_got, b_keep, *b_got], cuts)
    a_keep, a_send = parts[0], parts[1:ky]
    b_keep, b_send = parts[ky], parts[ky + 1 :]
    a_got = [across_group(v, 2 * (y + 1)) for y, v in enumerate(a_send)]
    b_got = [across_rep(v, x + 1) for x, v in enumerate(b_send)]
    na, nb = 1 + len(a_got), 1 + len(b_got)
    cuts = [
        [
            (0, m1, [(i, z * m1) for i in range(na)]),
            (m1, m2, [(na + i, z * m2) for i in range(nb)]),
        ]
        for z in range(kz)
    ]
    parts = cut([a_keep, *a_got, b_keep, *b_got], cuts)
    z_got = []
    for z in range(1, kz):
        z_got.append(across_rep(parts[z], 2 * z))
    mine = cut([parts[0], *z_got], [[(0, m1 + m2, [(i, 0) for i in range(kz)])]])[0]
    pieces = [mine] + [across_group(mine, t) for t in range(1, groups)]
    g_in, g_out, g_hot, g_mid, g_cold = call(
        functools.partial(final_body, plan, w_hot, w_mid, w_cold, cold_width),
        [
            sds((width, inner // reps), F32),
            sds((width // reps, inner), F32),
            sds((width // reps, w_hot), F32),
            sds((width // reps, w_mid), F32),
            sds((cold_width, width // reps), F32),
        ],
        pieces,
        scratch=[pltpu.VMEM((plan.rows, LANES), F32)],
        vmem=16,
    )

    q_keep, q_send = call(
        functools.partial(query_grad_body, groups),
        [sds((groups // 2, width, nq), BF16), sds((groups // 2, width, nq), BF16)],
        [vec, grad],
        vmem=16,
    )
    q_got = across_group(q_send, 1)
    own, *q_sends = call(
        query_core_body,
        [sds((width, nq), F32)] + [sds((width, nq), BF16)] * (ky - 1),
        [q_keep, q_got],
        vmem=16,
    )
    q_parts = [across_group(v, 2 * (y + 1)) for y, v in enumerate(q_sends)]
    query_grad = call(query_final_body, sds((nq, width), F32), [own, *q_parts], vmem=8)
    shapes = [table_hot.shape, table_mid.shape, table_cold.shape]
    o_hot, o_mid, o_cold = scatter_rows(served, back, proj_hot, shapes, cold_width)
    return (
        loss.reshape(nq),
        query_grad,
        o_hot,
        o_mid,
        o_cold,
        g_hot.T,
        g_mid.T,
        g_cold,
        g_in,
        g_out.T,
    )


def solution(mesh):
    split = P(AXES, None)
    deep = P(AXES, None, None)

    def body(*args):
        return local(mesh.shape["group"], mesh.shape["rep"], *args)

    return jax.shard_map(
        body,
        mesh=mesh,
        in_specs=(split, split, split, P(), P(), P(), P(), P(), split, P(AXES), deep, deep, deep),
        out_specs=(P(AXES), split, split, split, split) + (P(None, "rep"),) * 5,
        check_vma=False,
    )
```

profile of v0, /device:TPU:0, one launch (start us, length us, event | category | flops | bytes accessed | tf_op | source)
XLA Modules:
  0.0 96.2 jit_solution(9640083972925059365)
XLA Ops:
  0.7 3.5 %gather_rows.1 = bf16[256,768]{1,0:T(8,128)(2,1)} custom-call(s32[3,1,256]{2,1,0:T(1,128)} %bitcast.14, bf16[1024,512]{1,0:T(8,128)(2,1)} %hot.1, bf16[4096,128]{1,0:T(8,128)(2,1)} %mid.1, bf16[4096,128]{1,0:T(8,128)(2,1)} %cold.1), custom_call_target="tpu_custom_call" | custom-call | tf_op jit(solution)/shard_map/gather_rows/pallas_call | solution.py:112
  4.2 7.3 %all-to-all-start = ((bf16[32,8,768]{2,1,0:T(8,128)(2,1)}), bf16[32,8,768]{2,1,0:T(8,128)(2,1)S(1)}, u32[]{:S(2)}, u32[]{:S(2)}) async-start(bf16[32,8,768]{2,1,0:T(8,128)(2,1)} %bitcast.20), calls=%async_computation | async-start | bytes 786432 | tf_op jit(solution)/shard_map/all_to_all | solution.py:546
  11.6 1.8 %collective-permute-start.1 = (bf16[512,256]{1,0:T(8,128)(2,1)S(1)}, bf16[512,256]{1,0:T(8,128)(2,1)S(1)}, u32[]{:S(2)}, u32[]{:S(2)}) collective-permute-start(bf16[512,256]{1,0:T(8,128)(2,1)S(1)} %copy-done.5), channel_id=1, source_target_pairs={{0,16},{1,17},{2,18},{3,19},{4,20},{5,21},{6,22},{7,23},{8,24},{9,... | collective-permute-start | bytes 786440 | tf_op jit(solution)/shard_map/ppermute | solution.py:538
  13.4 10.8 %collective-permute-done.1.rest_2_.refs_6_ = bf16[512,256]{1,0:T(8,128)(2,1)S(1)} collective-permute-done((bf16[512,256]{1,0:T(8,128)(2,1)S(1)}, bf16[512,256]{1,0:T(8,128)(2,1)S(1)}, u32[]{:S(2)}, u32[]{:S(2)}) %collective-permute-start.1) | collective-permute-done | bytes 262176 | tf_op jit(solution)/shard_map/ppermute | solution.py:538
  25.3 2.5 %collective-permute-done.4.rest_6_.refs_10_ = s32[1,512]{1,0:T(1,128)S(1)} collective-permute-done((s32[1,512]{1,0:T(1,128)S(1)}, s32[1,512]{1,0:T(1,128)S(1)}, u32[]{:S(2)}, u32[]{:S(2)}) %collective-permute-start.4) | collective-permute-done | bytes 2080 | tf_op jit(solution)/shard_map/ppermute | solution.py:538
  27.8 5.7 %shard_map.204 = (bf16[1024,768]{1,0:T(8,128)(2,1)}, bf16[768,1024]{1,0:T(8,128)(2,1)}) custom-call(s32[1,4,1024]{2,1,0:T(4,128)} %item_slot.1, s32[1,4,1024]{2,1,0:T(4,128)} %item_block.1), custom_call_target="tpu_custom_call" | custom-call | tf_op jit(solution)/shard_map/pallas_call | solution.py:41
  33.6 1.4 %copy-done.3 = bf16[1024,768]{1,0:T(8,128)(2,1)S(1)} copy-done((bf16[1024,768]{1,0:T(8,128)(2,1)S(1)}, bf16[1024,768]{1,0:T(8,128)(2,1)}, u32[]{:S(2)}) %copy-start.3) | copy-done | bytes 1572888
  35.0 5.6 %shard_map.205 = (bf16[1024,256]{1,0:T(8,128)(2,1)S(1)}, f32[1024,256]{1,0:T(8,128)S(1)}, bf16[1024,256]{1,0:T(8,128)(2,1)S(1)}, f32[8,768]{1,0:T(8,128)S(1)}, f...) custom-call(bf16[256,768]{1,0:T(8,128)(2,1)S(1)} %bitcast.10, bf16[1024,768]{1,0:T(8,128)(2,1)S(1)} %copy-done.3, ...), custom_call_target="tpu_custom_call" | custom-call | tf_op jit(solution)/shard_map/pallas_call | solution.py:41
  41.7 1.2 %collective-permute-start.7 = (f32[8,768]{1,0:T(8,128)S(1)}, f32[8,768]{1,0:T(8,128)S(1)}, u32[]{:S(2)}, u32[]{:S(2)}) collective-permute-start(f32[8,768]{1,0:T(8,128)S(1)} %get-tuple-element.50.refs_0_), channel_id=1, source_target_pairs={{0,16},{1,17},{2,18},{3,19},{4,20},{5,21},{6,22},{7,23},{8,24},{9,... | collective-permute-start | bytes 73736 | tf_op jit(solution)/shard_map/ppermute | solution.py:538
  42.9 1.7 %shard_map.206 = (bf16[1024,1024]{1,0:T(8,128)(2,1)S(1)}, f32[1024,1024]{1,0:T(8,128)S(1)}) custom-call(bf16[1024,256]{1,0:T(8,128)(2,1)S(1)} %get-tuple-element.53.pooled.refs_17_, bf16[256,1024]{1,0:T(8,128)(2,1)S(1)} %copy-done), custom_call_target="tpu_custom_call" | custom-call | tf_op jit(solution)/shard_map/pallas_call | solution.py:41
  47.6 6.3 %shard_map.207 = (f32[1,512]{1,0:T(1,128)}, bf16[1024,2048]{1,0:T(8,128)(2,1)S(1)}, bf16[2816,128]{1,0:T(8,128)(2,1)S(1)}, bf16[2816,128]{1,0:T(8,128)(2,1)}, bf16[256,512]{1,0:T(8,128)(2,1)S(1)}) custom-call(f32[8,768]{1,0:T(8,128)S(1)} %get-tuple-element.50.refs_0_, f32[8,768]{1,0:T(8,128)S(1)} %collective-permute-done.6.refs_1_, ...), custom_call_target="tpu_custom_call" | custom-call | tf_op jit(solution)/shard_map/pallas_call | solution.py:41
  53.9 2.1 %shard_map.208 = (bf16[2,256,512]{2,1,0:T(8,128)(2,1)S(1)}, bf16[2,256,512]{2,1,0:T(8,128)(2,1)}) custom-call(bf16[1024,256]{1,0:T(8,128)(2,1)S(1)} %get-tuple-element.59.vec, bf16[1024,2048]{1,0:T(8,128)(2,1)S(1)} %get-tuple-element.60.grad), custom_call_target="tpu_custom_call" | custom-call | tf_op jit(solution)/shard_map/pallas_call | solution.py:41
  56.5 5.2 %all-to-all-start.1 = ((bf16[32,8,512]{2,1,0:T(8,128)(2,1)}), bf16[32,8,512]{2,1,0:T(8,128)(2,1)S(1)}, u32[]{:S(2)}, u32[]{:S(2)}) async-start(bf16[32,8,512]{2,1,0:T(8,128)(2,1)} %bitcast.13), calls=%async_computation.1 | async-start | bytes 524288 | tf_op jit(solution)/shard_map/all_to_all | solution.py:546
  61.9 1.8 %collective-permute-start.12 = (bf16[768,128]{1,0:T(8,128)(2,1)S(1)}, bf16[768,128]{1,0:T(8,128)(2,1)S(1)}, u32[]{:S(2)}, u32[]{:S(2)}) collective-permute-start(bf16[768,128]{1,0:T(8,128)(2,1)S(1)} %get-tuple-element.72), channel_id=1, source_target_pairs={{0,1},{1,0},{2,3},{3,2},{4,5},{5,4},{6,7},{7,6},{8,9},{9,8},{10,11... | collective-permute-start | bytes 589832 | tf_op jit(solution)/shard_map/ppermute | solution.py:542
  63.8 1.5 %collective-permute-start.13 = (bf16[640,128]{1,0:T(8,128)(2,1)S(1)}, bf16[640,128]{1,0:T(8,128)(2,1)S(1)}, u32[]{:S(2)}, u32[]{:S(2)}) collective-permute-start(bf16[640,128]{1,0:T(8,128)(2,1)S(1)} %get-tuple-element.74), channel_id=1, source_target_pairs={{0,16},{1,17},{2,18},{3,19},{4,20},{5,21},{6,22},{7,23},{8,24},{9,... | collective-permute-start | bytes 491528 | tf_op jit(solution)/shard_map/ppermute | solution.py:538
  67.8 4.4 %collective-permute-done.13.refs_3_ = bf16[640,128]{1,0:T(8,128)(2,1)S(1)} collective-permute-done((bf16[640,128]{1,0:T(8,128)(2,1)S(1)}, bf16[640,128]{1,0:T(8,128)(2,1)S(1)}, u32[]{:S(2)}, u32[]{:S(2)}) %collective-permute-start.13) | collective-permute-done | bytes 163872 | tf_op jit(solution)/shard_map/ppermute | solution.py:538
  72.3 1.2 %collective-permute-start.14 = (bf16[384,128]{1,0:T(8,128)(2,1)S(1)}, bf16[384,128]{1,0:T(8,128)(2,1)S(1)}, u32[]{:S(2)}, u32[]{:S(2)}) collective-permute-start(bf16[384,128]{1,0:T(8,128)(2,1)S(1)} %get-tuple-element.76), channel_id=1, source_target_pairs={{0,16},{1,17},{2,18},{3,19},{4,20},{5,21},{6,22},{7,23},{8,24},{9,... | collective-permute-start | bytes 294920 | tf_op jit(solution)/shard_map/ppermute | solution.py:538
  74.3 3.6 %collective-permute-done.15.refs_3_ = bf16[320,128]{1,0:T(8,128)(2,1)S(1)} collective-permute-done((bf16[320,128]{1,0:T(8,128)(2,1)S(1)}, bf16[320,128]{1,0:T(8,128)(2,1)S(1)}, u32[]{:S(2)}, u32[]{:S(2)}) %collective-permute-start.15) | collective-permute-done | bytes 81952 | tf_op jit(solution)/shard_map/ppermute | solution.py:542
  77.9 1.6 %collective-permute-done.14.refs_1_ = bf16[384,128]{1,0:T(8,128)(2,1)S(1)} collective-permute-done((bf16[384,128]{1,0:T(8,128)(2,1)S(1)}, bf16[384,128]{1,0:T(8,128)(2,1)S(1)}, u32[]{:S(2)}, u32[]{:S(2)}) %collective-permute-start.14) | collective-permute-done | bytes 98336 | tf_op jit(solution)/shard_map/ppermute | solution.py:538
  79.6 1.5 %collective-permute-start.16 = (bf16[176,128]{1,0:T(8,128)(2,1)S(1)}, bf16[176,128]{1,0:T(8,128)(2,1)S(1)}, u32[]{:S(2)}, u32[]{:S(2)}) collective-permute-start(bf16[176,128]{1,0:T(8,128)(2,1)S(1)} %get-tuple-element.80), channel_id=1, source_target_pairs={{0,2},{1,3},{2,0},{3,1},{4,6},{5,7},{6,4},{7,5},{8,10},{9,11},{10,... | collective-permute-start | bytes 135176 | tf_op jit(solution)/shard_map/ppermute | solution.py:542
  81.1 2.0 %collective-permute-start.17 = (bf16[176,128]{1,0:T(8,128)(2,1)S(1)}, bf16[176,128]{1,0:T(8,128)(2,1)S(1)}, u32[]{:S(2)}, u32[]{:S(2)}) collective-permute-start(bf16[176,128]{1,0:T(8,128)(2,1)S(1)} %get-tuple-element.81), channel_id=1, source_target_pairs={{0,4},{1,5},{2,6},{3,7},{4,0},{5,1},{6,2},{7,3},{8,12},{9,13},{10,... | collective-permute-start | bytes 135176 | tf_op jit(solution)/shard_map/ppermute | solution.py:542
  84.0 2.5 %collective-permute-done.17.refs_2_ = bf16[176,128]{1,0:T(8,128)(2,1)S(1)} collective-permute-done((bf16[176,128]{1,0:T(8,128)(2,1)S(1)}, bf16[176,128]{1,0:T(8,128)(2,1)S(1)}, u32[]{:S(2)}, u32[]{:S(2)}) %collective-permute-start.17) | collective-permute-done | bytes 45088 | tf_op jit(solution)/shard_map/ppermute | solution.py:542
  86.5 2.4 %collective-permute-done.18.refs_3_ = bf16[176,128]{1,0:T(8,128)(2,1)S(1)} collective-permute-done((bf16[176,128]{1,0:T(8,128)(2,1)S(1)}, bf16[176,128]{1,0:T(8,128)(2,1)S(1)}, u32[]{:S(2)}, u32[]{:S(2)}) %collective-permute-start.18) | collective-permute-done | bytes 45088 | tf_op jit(solution)/shard_map/ppermute | solution.py:542
  90.9 3.5 %scatter_rows.1 = (f32[1024,512]{1,0:T(8,128)}, f32[4096,128]{1,0:T(8,128)}, f32[4096,128]{1,0:T(8,128)}) custom-call(s32[3,1,256]{2,1,0:T(1,128)S(1)} %bitcast.15, bf16[256,512]{1,0:T(8,128)(2,1)S(1)} %bitcast.12, bf16[512,256]{1,0:T(8,128)(2,1)S(1)} %copy-done.1), custom_call_target="tpu_custom_call" | custom-call | tf_op jit(solution)/shard_map/scatter_rows/pallas_call | solution.py:495
  (78 shorter events, 14.1 us)
Async XLA Ops:
  4.2 29.3 %all-to-all-start = ((bf16[32,8,768]{2,1,0:T(8,128)(2,1)}), bf16[32,8,768]{2,1,0:T(8,128)(2,1)S(1)}, u32[]{:S(2)}, u32[]{:S(2)}) async-start(bf16[32,8,768]{2,1,0:T(8,128)(2,1)} %bitcast.20), calls=%async_computation | async-start | bytes 786432 | tf_op jit(solution)/shard_map/all_to_all | solution.py:546
  11.6 12.6 %collective-permute-start.1 = (bf16[512,256]{1,0:T(8,128)(2,1)S(1)}, bf16[512,256]{1,0:T(8,128)(2,1)S(1)}, u32[]{:S(2)}, u32[]{:S(2)}) collective-permute-start(bf16[512,256]{1,0:T(8,128)(2,1)S(1)} %copy-done.5), channel_id=1, source_target_pairs={{0,16},{1,17},{2,18},{3,19},{4,20},{5,21},{6,22},{7,23},{8,24},{9,... | collective-permute-start | bytes 786440 | tf_op jit(solution)/shard_map/ppermute | solution.py:538
  13.4 20.1 %collective-permute-start = (bf16[512,256]{1,0:T(8,128)(2,1)S(1)}, bf16[512,256]{1,0:T(8,128)(2,1)S(1)}, u32[]{:S(2)}, u32[]{:S(2)}) collective-permute-start(bf16[512,256]{1,0:T(8,128)(2,1)S(1)} %copy-done.5), channel_id=1, source_target_pairs={{0,8},{1,9},{2,10},{3,11},{4,12},{5,13},{6,14},{7,15},{8,0},{9,1},... | collective-permute-start | bytes 786440 | tf_op jit(solution)/shard_map/ppermute | solution.py:538
  24.2 9.4 %collective-permute-start.2 = (bf16[512,256]{1,0:T(8,128)(2,1)S(1)}, bf16[512,256]{1,0:T(8,128)(2,1)S(1)}, u32[]{:S(2)}, u32[]{:S(2)}) collective-permute-start(bf16[512,256]{1,0:T(8,128)(2,1)S(1)} %collective-permute-done.1.rest_2_.refs_6_), channel_id=1, source_target_pairs={{0,8},{1,9},{2,10},{3,11},{4,12},{5,13},{6,14},{7,15},{8,0},{9,1},... | collective-permute-start | bytes 786440 | tf_op jit(solution)/shard_map/ppermute | solution.py:538
  24.2 3.6 %collective-permute-start.4 = (s32[1,512]{1,0:T(1,128)S(1)}, s32[1,512]{1,0:T(1,128)S(1)}, u32[]{:S(2)}, u32[]{:S(2)}) collective-permute-start(s32[1,512]{1,0:T(1,128)S(1)} %bitcast.16), channel_id=1, source_target_pairs={{0,16},{1,17},{2,18},{3,19},{4,20},{5,21},{6,22},{7,23},{8,24},{9,... | collective-permute-start | bytes 6152 | tf_op jit(solution)/shard_map/ppermute | solution.py:538
  25.1 8.5 %collective-permute-start.3 = (s32[1,512]{1,0:T(1,128)S(1)}, s32[1,512]{1,0:T(1,128)S(1)}, u32[]{:S(2)}, u32[]{:S(2)}) collective-permute-start(s32[1,512]{1,0:T(1,128)S(1)} %bitcast.17), channel_id=1, source_target_pairs={{0,8},{1,9},{2,10},{3,11},{4,12},{5,13},{6,14},{7,15},{8,0},{9,1},... | collective-permute-start | bytes 6152 | tf_op jit(solution)/shard_map/ppermute | solution.py:538
  27.8 5.7 %collective-permute-start.5 = (s32[1,512]{1,0:T(1,128)S(1)}, s32[1,512]{1,0:T(1,128)S(1)}, u32[]{:S(2)}, u32[]{:S(2)}) collective-permute-start(s32[1,512]{1,0:T(1,128)S(1)} %collective-permute-done.4.rest_6_.refs_10_), channel_id=1, source_target_pairs={{0,8},{1,9},{2,10},{3,11},{4,12},{5,13},{6,14},{7,15},{8,0},{9,1},... | collective-permute-start | bytes 6152 | tf_op jit(solution)/shard_map/ppermute | solution.py:538
  40.7 3.9 %collective-permute-start.8 = (f32[8,768]{1,0:T(8,128)S(1)}, f32[8,768]{1,0:T(8,128)S(1)}, u32[]{:S(2)}, u32[]{:S(2)}) collective-permute-start(f32[8,768]{1,0:T(8,128)S(1)} %get-tuple-element.50.refs_0_), channel_id=1, source_target_pairs={{0,24},{1,25},{2,26},{3,27},{4,28},{5,29},{6,30},{7,31},{8,16},{9,... | collective-permute-start | bytes 73736 | tf_op jit(solution)/shard_map/ppermute | solution.py:538
  41.7 3.8 %collective-permute-start.7 = (f32[8,768]{1,0:T(8,128)S(1)}, f32[8,768]{1,0:T(8,128)S(1)}, u32[]{:S(2)}, u32[]{:S(2)}) collective-permute-start(f32[8,768]{1,0:T(8,128)S(1)} %get-tuple-element.50.refs_0_), channel_id=1, source_target_pairs={{0,16},{1,17},{2,18},{3,19},{4,20},{5,21},{6,22},{7,23},{8,24},{9,... | collective-permute-start | bytes 73736 | tf_op jit(solution)/shard_map/ppermute | solution.py:538
  42.9 2.7 %collective-permute-start.6 = (f32[8,768]{1,0:T(8,128)S(1)}, f32[8,768]{1,0:T(8,128)S(1)}, u32[]{:S(2)}, u32[]{:S(2)}) collective-permute-start(f32[8,768]{1,0:T(8,128)S(1)} %get-tuple-element.50.refs_0_), channel_id=1, source_target_pairs={{0,8},{1,9},{2,10},{3,11},{4,12},{5,13},{6,14},{7,15},{8,0},{9,1},... | collective-permute-start | bytes 73736 | tf_op jit(solution)/shard_map/ppermute | solution.py:538
  53.9 7.8 %collective-permute-start.11 = (bf16[2816,128]{1,0:T(8,128)(2,1)}, bf16[2816,128]{1,0:T(8,128)(2,1)S(1)}, u32[]{:S(2)}, u32[]{:S(2)}) collective-permute-start(bf16[2816,128]{1,0:T(8,128)(2,1)} %get-tuple-element.70), channel_id=1, source_target_pairs={{0,8},{1,9},{2,10},{3,11},{4,12},{5,13},{6,14},{7,15},{8,0},{9,1},... | collective-permute-start | bytes 2162696 | tf_op jit(solution)/shard_map/ppermute | solution.py:538
  56.0 9.3 %collective-permute-start.9 = (bf16[2,256,512]{2,1,0:T(8,128)(2,1)}, bf16[2,256,512]{2,1,0:T(8,128)(2,1)S(1)}, u32[]{:S(2)}, u32[]{:S(2)}) collective-permute-start(bf16[2,256,512]{2,1,0:T(8,128)(2,1)} %get-tuple-element.62), channel_id=1, source_target_pairs={{0,8},{1,9},{2,10},{3,11},{4,12},{5,13},{6,14},{7,15},{8,0},{9,1},... | collective-permute-start | bytes 1572872 | tf_op jit(solution)/shard_map/ppermute | solution.py:538
  56.5 34.4 %all-to-all-start.1 = ((bf16[32,8,512]{2,1,0:T(8,128)(2,1)}), bf16[32,8,512]{2,1,0:T(8,128)(2,1)S(1)}, u32[]{:S(2)}, u32[]{:S(2)}) async-start(bf16[32,8,512]{2,1,0:T(8,128)(2,1)} %bitcast.13), calls=%async_computation.1 | async-start | bytes 524288 | tf_op jit(solution)/shard_map/all_to_all | solution.py:546
  61.9 10.3 %collective-permute-start.12 = (bf16[768,128]{1,0:T(8,128)(2,1)S(1)}, bf16[768,128]{1,0:T(8,128)(2,1)S(1)}, u32[]{:S(2)}, u32[]{:S(2)}) collective-permute-start(bf16[768,128]{1,0:T(8,128)(2,1)S(1)} %get-tuple-element.72), channel_id=1, source_target_pairs={{0,1},{1,0},{2,3},{3,2},{4,5},{5,4},{6,7},{7,6},{8,9},{9,8},{10,11... | collective-permute-start | bytes 589832 | tf_op jit(solution)/shard_map/ppermute | solution.py:542
  63.8 8.5 %collective-permute-start.13 = (bf16[640,128]{1,0:T(8,128)(2,1)S(1)}, bf16[640,128]{1,0:T(8,128)(2,1)S(1)}, u32[]{:S(2)}, u32[]{:S(2)}) collective-permute-start(bf16[640,128]{1,0:T(8,128)(2,1)S(1)} %get-tuple-element.74), channel_id=1, source_target_pairs={{0,16},{1,17},{2,18},{3,19},{4,20},{5,21},{6,22},{7,23},{8,24},{9,... | collective-permute-start | bytes 491528 | tf_op jit(solution)/shard_map/ppermute | solution.py:538
  67.2 27.2 %collective-permute-start.10 = (bf16[256,512]{1,0:T(8,128)(2,1)S(1)}, bf16[256,512]{1,0:T(8,128)(2,1)S(1)}, u32[]{:S(2)}, u32[]{:S(2)}) collective-permute-start(bf16[256,512]{1,0:T(8,128)(2,1)S(1)} %get-tuple-element.64), channel_id=1, source_target_pairs={{0,16},{1,17},{2,18},{3,19},{4,20},{5,21},{6,22},{7,23},{8,24},{9,... | collective-permute-start | bytes 786440 | tf_op jit(solution)/shard_map/ppermute | solution.py:538
  72.3 7.2 %collective-permute-start.14 = (bf16[384,128]{1,0:T(8,128)(2,1)S(1)}, bf16[384,128]{1,0:T(8,128)(2,1)S(1)}, u32[]{:S(2)}, u32[]{:S(2)}) collective-permute-start(bf16[384,128]{1,0:T(8,128)(2,1)S(1)} %get-tuple-element.76), channel_id=1, source_target_pairs={{0,16},{1,17},{2,18},{3,19},{4,20},{5,21},{6,22},{7,23},{8,24},{9,... | collective-permute-start | bytes 294920 | tf_op jit(solution)/shard_map/ppermute | solution.py:538
  73.5 4.4 %collective-permute-start.15 = (bf16[320,128]{1,0:T(8,128)(2,1)S(1)}, bf16[320,128]{1,0:T(8,128)(2,1)S(1)}, u32[]{:S(2)}, u32[]{:S(2)}) collective-permute-start(bf16[320,128]{1,0:T(8,128)(2,1)S(1)} %get-tuple-element.78), channel_id=1, source_target_pairs={{0,1},{1,0},{2,3},{3,2},{4,5},{5,4},{6,7},{7,6},{8,9},{9,8},{10,11... | collective-permute-start | bytes 245768 | tf_op jit(solution)/shard_map/ppermute | solution.py:542
  79.6 4.5 %collective-permute-start.16 = (bf16[176,128]{1,0:T(8,128)(2,1)S(1)}, bf16[176,128]{1,0:T(8,128)(2,1)S(1)}, u32[]{:S(2)}, u32[]{:S(2)}) collective-permute-start(bf16[176,128]{1,0:T(8,128)(2,1)S(1)} %get-tuple-element.80), channel_id=1, source_target_pairs={{0,2},{1,3},{2,0},{3,1},{4,6},{5,7},{6,4},{7,5},{8,10},{9,11},{10,... | collective-permute-start | bytes 135176 | tf_op jit(solution)/shard_map/ppermute | solution.py:542
  81.1 5.4 %collective-permute-start.17 = (bf16[176,128]{1,0:T(8,128)(2,1)S(1)}, bf16[176,128]{1,0:T(8,128)(2,1)S(1)}, u32[]{:S(2)}, u32[]{:S(2)}) collective-permute-start(bf16[176,128]{1,0:T(8,128)(2,1)S(1)} %get-tuple-element.81), channel_id=1, source_target_pairs={{0,4},{1,5},{2,6},{3,7},{4,0},{5,1},{6,2},{7,3},{8,12},{9,13},{10,... | collective-permute-start | bytes 135176 | tf_op jit(solution)/shard_map/ppermute | solution.py:542
  83.1 5.8 %collective-permute-start.18 = (bf16[176,128]{1,0:T(8,128)(2,1)S(1)}, bf16[176,128]{1,0:T(8,128)(2,1)S(1)}, u32[]{:S(2)}, u32[]{:S(2)}) collective-permute-start(bf16[176,128]{1,0:T(8,128)(2,1)S(1)} %get-tuple-element.82), channel_id=1, source_target_pairs={{0,6},{1,7},{2,4},{3,5},{4,2},{5,3},{6,0},{7,1},{8,14},{9,15},{10,... | collective-permute-start | bytes 135176 | tf_op jit(solution)/shard_map/ppermute | solution.py:542
  88.9 6.4 %collective-permute-start.21 = (bf16[176,128]{1,0:T(8,128)(2,1)S(1)}, bf16[176,128]{1,0:T(8,128)(2,1)S(1)}, u32[]{:S(2)}, u32[]{:S(2)}) collective-permute-start(bf16[176,128]{1,0:T(8,128)(2,1)S(1)} %shard_map.214.refs_0_), channel_id=1, source_target_pairs={{0,24},{1,25},{2,26},{3,27},{4,28},{5,29},{6,30},{7,31},{8,16},{9,... | collective-permute-start | bytes 135176 | tf_op jit(solution)/shard_map/ppermute | solution.py:538
  89.0 6.3 %collective-permute-start.20 = (bf16[176,128]{1,0:T(8,128)(2,1)S(1)}, bf16[176,128]{1,0:T(8,128)(2,1)S(1)}, u32[]{:S(2)}, u32[]{:S(2)}) collective-permute-start(bf16[176,128]{1,0:T(8,128)(2,1)S(1)} %shard_map.214.refs_0_), channel_id=1, source_target_pairs={{0,16},{1,17},{2,18},{3,19},{4,20},{5,21},{6,22},{7,23},{8,24},{9,... | collective-permute-start | bytes 135176 | tf_op jit(solution)/shard_map/ppermute | solution.py:538
  89.9 5.4 %collective-permute-start.19 = (bf16[176,128]{1,0:T(8,128)(2,1)S(1)}, bf16[176,128]{1,0:T(8,128)(2,1)S(1)}, u32[]{:S(2)}, u32[]{:S(2)}) collective-permute-start(bf16[176,128]{1,0:T(8,128)(2,1)S(1)} %shard_map.214.refs_0_), channel_id=1, source_target_pairs={{0,8},{1,9},{2,10},{3,11},{4,12},{5,13},{6,14},{7,15},{8,0},{9,1},... | collective-permute-start | bytes 135176 | tf_op jit(solution)/shard_map/ppermute | solution.py:538
  (20 other events, 288.9 us)
where the time goes:
time: 96.8 us; the launch traced here: 96.2 us
  Pallas kernels  30.7 us (32%)
  starting transfers between devices  30.5 us (32%)
  waiting for transfers between devices  28.8 us (30%)
  local copies, waits for them, and re-layouts  5.34 us (6%)
    pallas_call x12, Pallas kernels, call(): pl.pallas_call(body, out_shape=out_shape, in_specs=[spec] * len(inputs) +...  23.7 us
    ppermute x17, waiting for transfers between devices, across_group(): return lax.ppermute(value, AXES, pairs)  20.2 us
    all_to_all x2, starting transfers between devices, to_all(): return lax.all_to_all(each, AXES, 0, 0, tiled=True).reshape(rows.shape)  12.6 us
    ppermute x17, starting transfers between devices, across_group(): return lax.ppermute(value, AXES, pairs)  10.8 us
    ppermute x5, waiting for transfers between devices, across_rep(): return lax.ppermute(value, AXES, pairs)  8.51 us
    ppermute x5, starting transfers between devices, across_rep(): return lax.ppermute(value, AXES, pairs)  7.11 us
    unnamed x40, local copies, waits for them, and re-layouts  5.34 us
    pallas_call x1, Pallas kernels, gather_rows(): pl.pallas_call(functools.partial(gather_body, cold_width, parts), out_sha...  3.52 us
  transfers between devices with their start and end apart: 24, of which 8 were waited for; matrix products, arithmetic and copies ran while one was open for 0% of the time, Pallas kernels for 15%

commit v1 on v0

--- a/solution.py
+++ b/solution.py
@@ -238,7 +238,8 @@
         stats_o[j : j + 1, 2 * QB :] = sum(part[2] for part in parts)
 
 
-def slope_body(pooled, t_in, hidden_o, slope_o):
+def slope_body(pooled, t_in, hidden_o, slope_o, turned_o):
+    turned_o[...] = pooled[...].T
     for at in range(0, pooled.shape[0], IB):
         rows = slice(at, at + IB)
         pre = mm(pooled[rows, :], t_in[...])
@@ -273,11 +274,11 @@
     stats, refs = refs[:peers], refs[peers:]
     queries, refs = refs[:peers], refs[peers:]
     labels, refs = refs[:peers], refs[peers:]
-    tops_r, grown, hidden, slope, resid, pooled, by_slot, raw = refs[:8]
+    tops_r, grown, hidden, slope, resid, turned, by_slot, raw = refs[:8]
     p_hot, p_mid, p_cold, t_in, t_out = refs[8:13]
     loss_o, grad_o, keep_o, send_o, back_o = refs[13:18]
     low_s, pre_s, pgrad_s, slot_s, chunk = refs[18:]
-    items, width = pooled.shape
+    width, items = turned.shape
     nq = queries[0].shape[0]
     per = nq // QB
     me_g, me_r = lax.axis_index("group"), lax.axis_index("rep")
@@ -327,7 +328,7 @@
         slot_s[2 * slots :, :], tall(p_cold[...], w_cold // p_cold.shape[0]), NT
     ).astype(BF16)
 
-    g_in = mm(pooled[...], pre_s[...], TN).T
+    g_in = mm(turned[...], pre_s[...]).T
     hr, dr = plan.hr, plan.dr
     for r in range(plan.reps):
         for b in range(plan.b_in):
@@ -583,9 +584,9 @@
     s_all = [stats]
     for t in range(1, groups):
         s_all.append(across_group(stats, t))
-    hidden, slope = call(
+    hidden, slope, turned = call(
         slope_body,
-        [sds((items, inner), BF16), sds((items, inner), F32)],
+        [sds((items, inner), BF16), sds((items, inner), F32), sds((width, items), BF16)],
         [pooled, tower_in],
         vmem=12,
     )
@@ -602,7 +603,7 @@
         s_all
         + q_all
         + l_all
-        + [tops, grown, hidden, slope, resid, pooled, by_slot, raw]
+        + [tops, grown, hidden, slope, resid, turned, by_slot, raw]
         + [proj_hot, proj_mid, proj_cold, tower_in, tower_out],
         scratch=[
             pltpu.VMEM((items, width), BF16),

time: 96.8 us -> 96.8 us (level)
  no operation moved by 1% of the time
where the time goes in v1:
time: 96.8 us; the launch traced here: 96.2 us
  Pallas kernels  30.7 us (32%)
  starting transfers between devices  30.5 us (32%)
  waiting for transfers between devices  28.7 us (30%)
  local copies, waits for them, and re-layouts  5.34 us (6%)
    pallas_call x12, Pallas kernels, call(): pl.pallas_call(body, out_shape=out_shape, in_specs=[spec] * len(inputs) +...  23.7 us
    ppermute x17, waiting for transfers between devices, across_group(): return lax.ppermute(value, AXES, pairs)  20.2 us
    all_to_all x2, starting transfers between devices, to_all(): return lax.all_to_all(each, AXES, 0, 0, tiled=True).reshape(rows.shape)  12.6 us
    ppermute x17, starting transfers between devices, across_group(): return lax.ppermute(value, AXES, pairs)  10.8 us
    ppermute x5, waiting for transfers between devices, across_rep(): return lax.ppermute(value, AXES, pairs)  8.51 us
    ppermute x5, starting transfers between devices, across_rep(): return lax.ppermute(value, AXES, pairs)  7.11 us
    unnamed x40, local copies, waits for them, and re-layouts  5.34 us
    pallas_call x1, Pallas kernels, gather_rows(): pl.pallas_call(functools.partial(gather_body, cold_width, parts), out_sha...  3.52 us
  transfers between devices with their start and end apart: 24, of which 8 were waited for; matrix products, arithmetic and copies ran while one was open for 0% of the time, Pallas kernels for 15%

profile of v1, /device:TPU:0, one launch (start us, length us, event | category | flops | bytes accessed | tf_op | source)
XLA Modules:
  0.0 96.2 jit_solution(1343550718456174344)
XLA Ops:
  0.7 3.5 %gather_rows.1 = bf16[256,768]{1,0:T(8,128)(2,1)} custom-call(s32[3,1,256]{2,1,0:T(1,128)} %bitcast.14, bf16[1024,512]{1,0:T(8,128)(2,1)} %hot.1, bf16[4096,128]{1,0:T(8,128)(2,1)} %mid.1, bf16[4096,128]{1,0:T(8,128)(2,1)} %cold.1), custom_call_target="tpu_custom_call" | custom-call | tf_op jit(solution)/shard_map/gather_rows/pallas_call | solution.py:112
  4.2 7.3 %all-to-all-start = ((bf16[32,8,768]{2,1,0:T(8,128)(2,1)}), bf16[32,8,768]{2,1,0:T(8,128)(2,1)S(1)}, u32[]{:S(2)}, u32[]{:S(2)}) async-start(bf16[32,8,768]{2,1,0:T(8,128)(2,1)} %bitcast.20), calls=%async_computation | async-start | bytes 786432 | tf_op jit(solution)/shard_map/all_to_all | solution.py:547
  11.6 1.8 %collective-permute-start.1 = (bf16[512,256]{1,0:T(8,128)(2,1)S(1)}, bf16[512,256]{1,0:T(8,128)(2,1)S(1)}, u32[]{:S(2)}, u32[]{:S(2)}) collective-permute-start(bf16[512,256]{1,0:T(8,128)(2,1)S(1)} %copy-done.5), channel_id=1, source_target_pairs={{0,16},{1,17},{2,18},{3,19},{4,20},{5,21},{6,22},{7,23},{8,24},{9,... | collective-permute-start | bytes 786440 | tf_op jit(solution)/shard_map/ppermute | solution.py:539
  13.4 10.8 %collective-permute-done.1.rest_2_.refs_6_ = bf16[512,256]{1,0:T(8,128)(2,1)S(1)} collective-permute-done((bf16[512,256]{1,0:T(8,128)(2,1)S(1)}, bf16[512,256]{1,0:T(8,128)(2,1)S(1)}, u32[]{:S(2)}, u32[]{:S(2)}) %collective-permute-start.1) | collective-permute-done | bytes 262176 | tf_op jit(solution)/shard_map/ppermute | solution.py:539
  25.3 2.5 %collective-permute-done.4.rest_6_.refs_10_ = s32[1,512]{1,0:T(1,128)S(1)} collective-permute-done((s32[1,512]{1,0:T(1,128)S(1)}, s32[1,512]{1,0:T(1,128)S(1)}, u32[]{:S(2)}, u32[]{:S(2)}) %collective-permute-start.4) | collective-permute-done | bytes 2080 | tf_op jit(solution)/shard_map/ppermute | solution.py:539
  27.8 5.7 %shard_map.204 = (bf16[1024,768]{1,0:T(8,128)(2,1)}, bf16[768,1024]{1,0:T(8,128)(2,1)}) custom-call(s32[1,4,1024]{2,1,0:T(4,128)} %item_slot.1, s32[1,4,1024]{2,1,0:T(4,128)} %item_block.1), custom_call_target="tpu_custom_call" | custom-call | tf_op jit(solution)/shard_map/pallas_call | solution.py:41
  33.6 1.4 %copy-done.3 = bf16[1024,768]{1,0:T(8,128)(2,1)S(1)} copy-done((bf16[1024,768]{1,0:T(8,128)(2,1)S(1)}, bf16[1024,768]{1,0:T(8,128)(2,1)}, u32[]{:S(2)}) %copy-start.3) | copy-done | bytes 1572888
  35.0 5.6 %shard_map.205 = (bf16[1024,256]{1,0:T(8,128)(2,1)S(1)}, f32[1024,256]{1,0:T(8,128)S(1)}, bf16[1024,256]{1,0:T(8,128)(2,1)S(1)}, f32[8,768]{1,0:T(8,128)S(1)}, f...) custom-call(bf16[256,768]{1,0:T(8,128)(2,1)S(1)} %bitcast.10, bf16[1024,768]{1,0:T(8,128)(2,1)S(1)} %copy-done.3, ...), custom_call_target="tpu_custom_call" | custom-call | tf_op jit(solution)/shard_map/pallas_call | solution.py:41
  41.7 1.2 %collective-permute-start.7 = (f32[8,768]{1,0:T(8,128)S(1)}, f32[8,768]{1,0:T(8,128)S(1)}, u32[]{:S(2)}, u32[]{:S(2)}) collective-permute-start(f32[8,768]{1,0:T(8,128)S(1)} %get-tuple-element.51.refs_0_), channel_id=1, source_target_pairs={{0,16},{1,17},{2,18},{3,19},{4,20},{5,21},{6,22},{7,23},{8,24},{9,... | collective-permute-start | bytes 73736 | tf_op jit(solution)/shard_map/ppermute | solution.py:539
  42.9 1.7 %shard_map.206 = (bf16[1024,1024]{1,0:T(8,128)(2,1)S(1)}, f32[1024,1024]{1,0:T(8,128)S(1)}, bf16[256,1024]{1,0:T(8,128)(2,1)S(1)}) custom-call(bf16[1024,256]{1,0:T(8,128)(2,1)S(1)} %get-tuple-element.54.pooled, bf16[256,1024]{1,0:T(8,128)(2,1)S(1)} %copy-done), custom_call_target="tpu_custom_call" | custom-call | tf_op jit(solution)/shard_map/pallas_call | solution.py:41
  47.6 6.3 %shard_map.207 = (f32[1,512]{1,0:T(1,128)}, bf16[1024,2048]{1,0:T(8,128)(2,1)S(1)}, bf16[2816,128]{1,0:T(8,128)(2,1)S(1)}, bf16[2816,128]{1,0:T(8,128)(2,1)}, bf16[256,512]{1,0:T(8,128)(2,1)S(1)}) custom-call(f32[8,768]{1,0:T(8,128)S(1)} %get-tuple-element.51.refs_0_, f32[8,768]{1,0:T(8,128)S(1)} %collective-permute-done.6.refs_1_, ...), custom_call_target="tpu_custom_call" | custom-call | tf_op jit(solution)/shard_map/pallas_call | solution.py:41
  53.9 2.1 %shard_map.208 = (bf16[2,256,512]{2,1,0:T(8,128)(2,1)S(1)}, bf16[2,256,512]{2,1,0:T(8,128)(2,1)}) custom-call(bf16[1024,256]{1,0:T(8,128)(2,1)S(1)} %get-tuple-element.61.vec, bf16[1024,2048]{1,0:T(8,128)(2,1)S(1)} %get-tuple-element.62.grad), custom_call_target="tpu_custom_call" | custom-call | tf_op jit(solution)/shard_map/pallas_call | solution.py:41
  56.5 5.2 %all-to-all-start.1 = ((bf16[32,8,512]{2,1,0:T(8,128)(2,1)}), bf16[32,8,512]{2,1,0:T(8,128)(2,1)S(1)}, u32[]{:S(2)}, u32[]{:S(2)}) async-start(bf16[32,8,512]{2,1,0:T(8,128)(2,1)} %bitcast.13), calls=%async_computation.1 | async-start | bytes 524288 | tf_op jit(solution)/shard_map/all_to_all | solution.py:547
  61.9 1.8 %collective-permute-start.12 = (bf16[768,128]{1,0:T(8,128)(2,1)S(1)}, bf16[768,128]{1,0:T(8,128)(2,1)S(1)}, u32[]{:S(2)}, u32[]{:S(2)}) collective-permute-start(bf16[768,128]{1,0:T(8,128)(2,1)S(1)} %get-tuple-element.74), channel_id=1, source_target_pairs={{0,1},{1,0},{2,3},{3,2},{4,5},{5,4},{6,7},{7,6},{8,9},{9,8},{10,11... | collective-permute-start | bytes 589832 | tf_op jit(solution)/shard_map/ppermute | solution.py:543
  63.8 1.5 %collective-permute-start.13 = (bf16[640,128]{1,0:T(8,128)(2,1)S(1)}, bf16[640,128]{1,0:T(8,128)(2,1)S(1)}, u32[]{:S(2)}, u32[]{:S(2)}) collective-permute-start(bf16[640,128]{1,0:T(8,128)(2,1)S(1)} %get-tuple-element.76), channel_id=1, source_target_pairs={{0,16},{1,17},{2,18},{3,19},{4,20},{5,21},{6,22},{7,23},{8,24},{9,... | collective-permute-start | bytes 491528 | tf_op jit(solution)/shard_map/ppermute | solution.py:539
  67.8 4.4 %collective-permute-done.13.refs_3_ = bf16[640,128]{1,0:T(8,128)(2,1)S(1)} collective-permute-done((bf16[640,128]{1,0:T(8,128)(2,1)S(1)}, bf16[640,128]{1,0:T(8,128)(2,1)S(1)}, u32[]{:S(2)}, u32[]{:S(2)}) %collective-permute-start.13) | collective-permute-done | bytes 163872 | tf_op jit(solution)/shard_map/ppermute | solution.py:539
  72.3 1.2 %collective-permute-start.14 = (bf16[384,128]{1,0:T(8,128)(2,1)S(1)}, bf16[384,128]{1,0:T(8,128)(2,1)S(1)}, u32[]{:S(2)}, u32[]{:S(2)}) collective-permute-start(bf16[384,128]{1,0:T(8,128)(2,1)S(1)} %get-tuple-element.78), channel_id=1, source_target_pairs={{0,16},{1,17},{2,18},{3,19},{4,20},{5,21},{6,22},{7,23},{8,24},{9,... | collective-permute-start | bytes 294920 | tf_op jit(solution)/shard_map/ppermute | solution.py:539
  74.3 3.6 %collective-permute-done.15.refs_3_ = bf16[320,128]{1,0:T(8,128)(2,1)S(1)} collective-permute-done((bf16[320,128]{1,0:T(8,128)(2,1)S(1)}, bf16[320,128]{1,0:T(8,128)(2,1)S(1)}, u32[]{:S(2)}, u32[]{:S(2)}) %collective-permute-start.15) | collective-permute-done | bytes 81952 | tf_op jit(solution)/shard_map/ppermute | solution.py:543
  77.9 1.6 %collective-permute-done.14.refs_1_ = bf16[384,128]{1,0:T(8,128)(2,1)S(1)} collective-permute-done((bf16[384,128]{1,0:T(8,128)(2,1)S(1)}, bf16[384,128]{1,0:T(8,128)(2,1)S(1)}, u32[]{:S(2)}, u32[]{:S(2)}) %collective-permute-start.14) | collective-permute-done | bytes 98336 | tf_op jit(solution)/shard_map/ppermute | solution.py:539
  79.6 1.5 %collective-permute-start.16 = (bf16[176,128]{1,0:T(8,128)(2,1)S(1)}, bf16[176,128]{1,0:T(8,128)(2,1)S(1)}, u32[]{:S(2)}, u32[]{:S(2)}) collective-permute-start(bf16[176,128]{1,0:T(8,128)(2,1)S(1)} %get-tuple-element.82), channel_id=1, source_target_pairs={{0,2},{1,3},{2,0},{3,1},{4,6},{5,7},{6,4},{7,5},{8,10},{9,11},{10,... | collective-permute-start | bytes 135176 | tf_op jit(solution)/shard_map/ppermute | solution.py:543
  81.1 2.0 %collective-permute-start.17 = (bf16[176,128]{1,0:T(8,128)(2,1)S(1)}, bf16[176,128]{1,0:T(8,128)(2,1)S(1)}, u32[]{:S(2)}, u32[]{:S(2)}) collective-permute-start(bf16[176,128]{1,0:T(8,128)(2,1)S(1)} %get-tuple-element.83), channel_id=1, source_target_pairs={{0,4},{1,5},{2,6},{3,7},{4,0},{5,1},{6,2},{7,3},{8,12},{9,13},{10,... | collective-permute-start | bytes 135176 | tf_op jit(solution)/shard_map/ppermute | solution.py:543
  84.0 2.5 %collective-permute-done.17.refs_2_ = bf16[176,128]{1,0:T(8,128)(2,1)S(1)} collective-permute-done((bf16[176,128]{1,0:T(8,128)(2,1)S(1)}, bf16[176,128]{1,0:T(8,128)(2,1)S(1)}, u32[]{:S(2)}, u32[]{:S(2)}) %collective-permute-start.17) | collective-permute-done | bytes 45088 | tf_op jit(solution)/shard_map/ppermute | solution.py:543
  86.5 2.4 %collective-permute-done.18.refs_3_ = bf16[176,128]{1,0:T(8,128)(2,1)S(1)} collective-permute-done((bf16[176,128]{1,0:T(8,128)(2,1)S(1)}, bf16[176,128]{1,0:T(8,128)(2,1)S(1)}, u32[]{:S(2)}, u32[]{:S(2)}) %collective-permute-start.18) | collective-permute-done | bytes 45088 | tf_op jit(solution)/shard_map/ppermute | solution.py:543
  90.9 3.5 %scatter_rows.1 = (f32[1024,512]{1,0:T(8,128)}, f32[4096,128]{1,0:T(8,128)}, f32[4096,128]{1,0:T(8,128)}) custom-call(s32[3,1,256]{2,1,0:T(1,128)S(1)} %bitcast.15, bf16[256,512]{1,0:T(8,128)(2,1)S(1)} %bitcast.12, bf16[512,256]{1,0:T(8,128)(2,1)S(1)} %copy-done.1), custom_call_target="tpu_custom_call" | custom-call | tf_op jit(solution)/shard_map/scatter_rows/pallas_call | solution.py:496
  (78 shorter events, 14.1 us)
Async XLA Ops:
  4.2 29.3 %all-to-all-start = ((bf16[32,8,768]{2,1,0:T(8,128)(2,1)}), bf16[32,8,768]{2,1,0:T(8,128)(2,1)S(1)}, u32[]{:S(2)}, u32[]{:S(2)}) async-start(bf16[32,8,768]{2,1,0:T(8,128)(2,1)} %bitcast.20), calls=%async_computation | async-start | bytes 786432 | tf_op jit(solution)/shard_map/all_to_all | solution.py:547
  11.6 12.6 %collective-permute-start.1 = (bf16[512,256]{1,0:T(8,128)(2,1)S(1)}, bf16[512,256]{1,0:T(8,128)(2,1)S(1)}, u32[]{:S(2)}, u32[]{:S(2)}) collective-permute-start(bf16[512,256]{1,0:T(8,128)(2,1)S(1)} %copy-done.5), channel_id=1, source_target_pairs={{0,16},{1,17},{2,18},{3,19},{4,20},{5,21},{6,22},{7,23},{8,24},{9,... | collective-permute-start | bytes 786440 | tf_op jit(solution)/shard_map/ppermute | solution.py:539
  13.4 20.1 %collective-permute-start = (bf16[512,256]{1,0:T(8,128)(2,1)S(1)}, bf16[512,256]{1,0:T(8,128)(2,1)S(1)}, u32[]{:S(2)}, u32[]{:S(2)}) collective-permute-start(bf16[512,256]{1,0:T(8,128)(2,1)S(1)} %copy-done.5), channel_id=1, source_target_pairs={{0,8},{1,9},{2,10},{3,11},{4,12},{5,13},{6,14},{7,15},{8,0},{9,1},... | collective-permute-start | bytes 786440 | tf_op jit(solution)/shard_map/ppermute | solution.py:539
  24.2 9.4 %collective-permute-start.2 = (bf16[512,256]{1,0:T(8,128)(2,1)S(1)}, bf16[512,256]{1,0:T(8,128)(2,1)S(1)}, u32[]{:S(2)}, u32[]{:S(2)}) collective-permute-start(bf16[512,256]{1,0:T(8,128)(2,1)S(1)} %collective-permute-done.1.rest_2_.refs_6_), channel_id=1, source_target_pairs={{0,8},{1,9},{2,10},{3,11},{4,12},{5,13},{6,14},{7,15},{8,0},{9,1},... | collective-permute-start | bytes 786440 | tf_op jit(solution)/shard_map/ppermute | solution.py:539
  24.2 3.6 %collective-permute-start.4 = (s32[1,512]{1,0:T(1,128)S(1)}, s32[1,512]{1,0:T(1,128)S(1)}, u32[]{:S(2)}, u32[]{:S(2)}) collective-permute-start(s32[1,512]{1,0:T(1,128)S(1)} %bitcast.16), channel_id=1, source_target_pairs={{0,16},{1,17},{2,18},{3,19},{4,20},{5,21},{6,22},{7,23},{8,24},{9,... | collective-permute-start | bytes 6152 | tf_op jit(solution)/shard_map/ppermute | solution.py:539
  25.1 8.5 %collective-permute-start.3 = (s32[1,512]{1,0:T(1,128)S(1)}, s32[1,512]{1,0:T(1,128)S(1)}, u32[]{:S(2)}, u32[]{:S(2)}) collective-permute-start(s32[1,512]{1,0:T(1,128)S(1)} %bitcast.17), channel_id=1, source_target_pairs={{0,8},{1,9},{2,10},{3,11},{4,12},{5,13},{6,14},{7,15},{8,0},{9,1},... | collective-permute-start | bytes 6152 | tf_op jit(solution)/shard_map/ppermute | solution.py:539
  27.8 5.7 %collective-permute-start.5 = (s32[1,512]{1,0:T(1,128)S(1)}, s32[1,512]{1,0:T(1,128)S(1)}, u32[]{:S(2)}, u32[]{:S(2)}) collective-permute-start(s32[1,512]{1,0:T(1,128)S(1)} %collective-permute-done.4.rest_6_.refs_10_), channel_id=1, source_target_pairs={{0,8},{1,9},{2,10},{3,11},{4,12},{5,13},{6,14},{7,15},{8,0},{9,1},... | collective-permute-start | bytes 6152 | tf_op jit(solution)/shard_map/ppermute | solution.py:539
  40.7 3.9 %collective-permute-start.8 = (f32[8,768]{1,0:T(8,128)S(1)}, f32[8,768]{1,0:T(8,128)S(1)}, u32[]{:S(2)}, u32[]{:S(2)}) collective-permute-start(f32[8,768]{1,0:T(8,128)S(1)} %get-tuple-element.51.refs_0_), channel_id=1, source_target_pairs={{0,24},{1,25},{2,26},{3,27},{4,28},{5,29},{6,30},{7,31},{8,16},{9,... | collective-permute-start | bytes 73736 | tf_op jit(solution)/shard_map/ppermute | solution.py:539
  41.7 3.8 %collective-permute-start.7 = (f32[8,768]{1,0:T(8,128)S(1)}, f32[8,768]{1,0:T(8,128)S(1)}, u32[]{:S(2)}, u32[]{:S(2)}) collective-permute-start(f32[8,768]{1,0:T(8,128)S(1)} %get-tuple-element.51.refs_0_), channel_id=1, source_target_pairs={{0,16},{1,17},{2,18},{3,19},{4,20},{5,21},{6,22},{7,23},{8,24},{9,... | collective-permute-start | bytes 73736 | tf_op jit(solution)/shard_map/ppermute | solution.py:539
  42.9 2.7 %collective-permute-start.6 = (f32[8,768]{1,0:T(8,128)S(1)}, f32[8,768]{1,0:T(8,128)S(1)}, u32[]{:S(2)}, u32[]{:S(2)}) collective-permute-start(f32[8,768]{1,0:T(8,128)S(1)} %get-tuple-element.51.refs_0_), channel_id=1, source_target_pairs={{0,8},{1,9},{2,10},{3,11},{4,12},{5,13},{6,14},{7,15},{8,0},{9,1},... | collective-permute-start | bytes 73736 | tf_op jit(solution)/shard_map/ppermute | solution.py:539
  53.9 7.8 %collective-permute-start.11 = (bf16[2816,128]{1,0:T(8,128)(2,1)}, bf16[2816,128]{1,0:T(8,128)(2,1)S(1)}, u32[]{:S(2)}, u32[]{:S(2)}) collective-permute-start(bf16[2816,128]{1,0:T(8,128)(2,1)} %get-tuple-element.72), channel_id=1, source_target_pairs={{0,8},{1,9},{2,10},{3,11},{4,12},{5,13},{6,14},{7,15},{8,0},{9,1},... | collective-permute-start | bytes 2162696 | tf_op jit(solution)/shard_map/ppermute | solution.py:539
  56.0 9.2 %collective-permute-start.9 = (bf16[2,256,512]{2,1,0:T(8,128)(2,1)}, bf16[2,256,512]{2,1,0:T(8,128)(2,1)S(1)}, u32[]{:S(2)}, u32[]{:S(2)}) collective-permute-start(bf16[2,256,512]{2,1,0:T(8,128)(2,1)} %get-tuple-element.64), channel_id=1, source_target_pairs={{0,8},{1,9},{2,10},{3,11},{4,12},{5,13},{6,14},{7,15},{8,0},{9,1},... | collective-permute-start | bytes 1572872 | tf_op jit(solution)/shard_map/ppermute | solution.py:539
  56.5 34.4 %all-to-all-start.1 = ((bf16[32,8,512]{2,1,0:T(8,128)(2,1)}), bf16[32,8,512]{2,1,0:T(8,128)(2,1)S(1)}, u32[]{:S(2)}, u32[]{:S(2)}) async-start(bf16[32,8,512]{2,1,0:T(8,128)(2,1)} %bitcast.13), calls=%async_computation.1 | async-start | bytes 524288 | tf_op jit(solution)/shard_map/all_to_all | solution.py:547
  61.9 10.3 %collective-permute-start.12 = (bf16[768,128]{1,0:T(8,128)(2,1)S(1)}, bf16[768,128]{1,0:T(8,128)(2,1)S(1)}, u32[]{:S(2)}, u32[]{:S(2)}) collective-permute-start(bf16[768,128]{1,0:T(8,128)(2,1)S(1)} %get-tuple-element.74), channel_id=1, source_target_pairs={{0,1},{1,0},{2,3},{3,2},{4,5},{5,4},{6,7},{7,6},{8,9},{9,8},{10,11... | collective-permute-start | bytes 589832 | tf_op jit(solution)/shard_map/ppermute | solution.py:543
  63.8 8.5 %collective-permute-start.13 = (bf16[640,128]{1,0:T(8,128)(2,1)S(1)}, bf16[640,128]{1,0:T(8,128)(2,1)S(1)}, u32[]{:S(2)}, u32[]{:S(2)}) collective-permute-start(bf16[640,128]{1,0:T(8,128)(2,1)S(1)} %get-tuple-element.76), channel_id=1, source_target_pairs={{0,16},{1,17},{2,18},{3,19},{4,20},{5,21},{6,22},{7,23},{8,24},{9,... | collective-permute-start | bytes 491528 | tf_op jit(solution)/shard_map/ppermute | solution.py:539
  67.2 27.2 %collective-permute-start.10 = (bf16[256,512]{1,0:T(8,128)(2,1)S(1)}, bf16[256,512]{1,0:T(8,128)(2,1)S(1)}, u32[]{:S(2)}, u32[]{:S(2)}) collective-permute-start(bf16[256,512]{1,0:T(8,128)(2,1)S(1)} %get-tuple-element.66), channel_id=1, source_target_pairs={{0,16},{1,17},{2,18},{3,19},{4,20},{5,21},{6,22},{7,23},{8,24},{9,... | collective-permute-start | bytes 786440 | tf_op jit(solution)/shard_map/ppermute | solution.py:539
  72.3 7.2 %collective-permute-start.14 = (bf16[384,128]{1,0:T(8,128)(2,1)S(1)}, bf16[384,128]{1,0:T(8,128)(2,1)S(1)}, u32[]{:S(2)}, u32[]{:S(2)}) collective-permute-start(bf16[384,128]{1,0:T(8,128)(2,1)S(1)} %get-tuple-element.78), channel_id=1, source_target_pairs={{0,16},{1,17},{2,18},{3,19},{4,20},{5,21},{6,22},{7,23},{8,24},{9,... | collective-permute-start | bytes 294920 | tf_op jit(solution)/shard_map/ppermute | solution.py:539
  73.5 4.4 %collective-permute-start.15 = (bf16[320,128]{1,0:T(8,128)(2,1)S(1)}, bf16[320,128]{1,0:T(8,128)(2,1)S(1)}, u32[]{:S(2)}, u32[]{:S(2)}) collective-permute-start(bf16[320,128]{1,0:T(8,128)(2,1)S(1)} %get-tuple-element.80), channel_id=1, source_target_pairs={{0,1},{1,0},{2,3},{3,2},{4,5},{5,4},{6,7},{7,6},{8,9},{9,8},{10,11... | collective-permute-start | bytes 245768 | tf_op jit(solution)/shard_map/ppermute | solution.py:543
  79.6 4.5 %collective-permute-start.16 = (bf16[176,128]{1,0:T(8,128)(2,1)S(1)}, bf16[176,128]{1,0:T(8,128)(2,1)S(1)}, u32[]{:S(2)}, u32[]{:S(2)}) collective-permute-start(bf16[176,128]{1,0:T(8,128)(2,1)S(1)} %get-tuple-element.82), channel_id=1, source_target_pairs={{0,2},{1,3},{2,0},{3,1},{4,6},{5,7},{6,4},{7,5},{8,10},{9,11},{10,... | collective-permute-start | bytes 135176 | tf_op jit(solution)/shard_map/ppermute | solution.py:543
  81.1 5.4 %collective-permute-start.17 = (bf16[176,128]{1,0:T(8,128)(2,1)S(1)}, bf16[176,128]{1,0:T(8,128)(2,1)S(1)}, u32[]{:S(2)}, u32[]{:S(2)}) collective-permute-start(bf16[176,128]{1,0:T(8,128)(2,1)S(1)} %get-tuple-element.83), channel_id=1, source_target_pairs={{0,4},{1,5},{2,6},{3,7},{4,0},{5,1},{6,2},{7,3},{8,12},{9,13},{10,... | collective-permute-start | bytes 135176 | tf_op jit(solution)/shard_map/ppermute | solution.py:543
  83.1 5.8 %collective-permute-start.18 = (bf16[176,128]{1,0:T(8,128)(2,1)S(1)}, bf16[176,128]{1,0:T(8,128)(2,1)S(1)}, u32[]{:S(2)}, u32[]{:S(2)}) collective-permute-start(bf16[176,128]{1,0:T(8,128)(2,1)S(1)} %get-tuple-element.84), channel_id=1, source_target_pairs={{0,6},{1,7},{2,4},{3,5},{4,2},{5,3},{6,0},{7,1},{8,14},{9,15},{10,... | collective-permute-start | bytes 135176 | tf_op jit(solution)/shard_map/ppermute | solution.py:543
  88.9 6.4 %collective-permute-start.21 = (bf16[176,128]{1,0:T(8,128)(2,1)S(1)}, bf16[176,128]{1,0:T(8,128)(2,1)S(1)}, u32[]{:S(2)}, u32[]{:S(2)}) collective-permute-start(bf16[176,128]{1,0:T(8,128)(2,1)S(1)} %shard_map.214.refs_0_), channel_id=1, source_target_pairs={{0,24},{1,25},{2,26},{3,27},{4,28},{5,29},{6,30},{7,31},{8,16},{9,... | collective-permute-start | bytes 135176 | tf_op jit(solution)/shard_map/ppermute | solution.py:539
  89.0 6.3 %collective-permute-start.20 = (bf16[176,128]{1,0:T(8,128)(2,1)S(1)}, bf16[176,128]{1,0:T(8,128)(2,1)S(1)}, u32[]{:S(2)}, u32[]{:S(2)}) collective-permute-start(bf16[176,128]{1,0:T(8,128)(2,1)S(1)} %shard_map.214.refs_0_), channel_id=1, source_target_pairs={{0,16},{1,17},{2,18},{3,19},{4,20},{5,21},{6,22},{7,23},{8,24},{9,... | collective-permute-start | bytes 135176 | tf_op jit(solution)/shard_map/ppermute | solution.py:539
  89.9 5.4 %collective-permute-start.19 = (bf16[176,128]{1,0:T(8,128)(2,1)S(1)}, bf16[176,128]{1,0:T(8,128)(2,1)S(1)}, u32[]{:S(2)}, u32[]{:S(2)}) collective-permute-start(bf16[176,128]{1,0:T(8,128)(2,1)S(1)} %shard_map.214.refs_0_), channel_id=1, source_target_pairs={{0,8},{1,9},{2,10},{3,11},{4,12},{5,13},{6,14},{7,15},{8,0},{9,1},... | collective-permute-start | bytes 135176 | tf_op jit(solution)/shard_map/ppermute | solution.py:539
  (20 other events, 288.9 us)
